TPU v7x, 32 devices: a whole 2x2x4 slice. The times are simulated.
32 devices in a mesh: dp: 8 (over z, y), tensor: 4 (over x, core).
Axes of the slice: x: 2, y: 2, z: 4, core: 2. Of those that a mesh axis runs over, the one named last changes fastest.
Arguments:
- inputs: bfloat16 [8, 1024, 2048], P('dp', 'tensor'), may hold values from -6 to 6
- cotangent: bfloat16 [8, 1024, 2048], P('dp', 'tensor'), may hold values from -6 to 6
- lengths: int32 [8], P('dp'), may hold values from 256 to 1024, as said below
- norm1_gain: float32 [2048], replicated, may hold values from 0.5 to 1.5
- w_query: bfloat16 [2048, 2048], P('dp', 'tensor'), may hold values from -0.125 to 0.125
- w_key: bfloat16 [2048, 2048], P('dp', 'tensor'), may hold values from -0.125 to 0.125
- w_value: bfloat16 [2048, 4096], P('dp', 'tensor'), may hold values from -0.125 to 0.125
- w_outgate: bfloat16 [2048, 4096], P('dp', 'tensor'), may hold values from -0.125 to 0.125
- w_beta: bfloat16 [2048, 16], P('dp', 'tensor'), may hold values from -0.125 to 0.125
- w_alpha: bfloat16 [2048, 16], P('dp', 'tensor'), may hold values from -0.125 to 0.125
- conv_query: bfloat16 [128, 16, 4], P('dp', 'tensor'), may hold values from -3 to 3
- conv_key: bfloat16 [128, 16, 4], P('dp', 'tensor'), may hold values from -3 to 3
- conv_value: bfloat16 [256, 16, 4], P('dp', 'tensor'), may hold values from -3 to 3
- a_log: float32 [16], replicated, may hold values from -6.5 to -3
- dt_bias: float32 [16], replicated, may hold values from -1.5 to 0.5
- head_gain: float32 [256], replicated, may hold values from 0.5 to 1.5
- w_out: bfloat16 [2048, 4096], P('dp', 'tensor'), may hold values from -0.125 to 0.125
- norm2_gain: float32 [2048], replicated, may hold values from 0.5 to 1.5
- w_gate: bfloat16 [2048, 5632], P('dp', 'tensor'), may hold values from -0.125 to 0.125
- w_up: bfloat16 [2048, 5632], P('dp', 'tensor'), may hold values from -0.125 to 0.125
- w_down: bfloat16 [2048, 5632], P('dp', 'tensor'), may hold values from -0.109375 to 0.109375
Outputs:
- outputs: bfloat16 [8, 1024, 2048], P('dp', 'tensor')
- grad_inputs: float32 [8, 1024, 2048], P('dp', 'tensor')
- grad_norm1: float32 [2048], replicated
- grad_query: float32 [2048, 2048], P('dp', 'tensor')
- grad_key: float32 [2048, 2048], P('dp', 'tensor')
- grad_value: float32 [2048, 4096], P('dp', 'tensor')
- grad_outgate: float32 [2048, 4096], P('dp', 'tensor')
- grad_beta: float32 [2048, 16], P('dp', 'tensor')
- grad_alpha: float32 [2048, 16], P('dp', 'tensor')
- grad_convq: float32 [128, 16, 4], P('dp', 'tensor')
- grad_convk: float32 [128, 16, 4], P('dp', 'tensor')
- grad_convv: float32 [256, 16, 4], P('dp', 'tensor')
- grad_alog: float32 [16], replicated
- grad_dtbias: float32 [16], replicated
- grad_headgain: float32 [256], replicated
- grad_out: float32 [2048, 4096], P('dp', 'tensor')
- grad_norm2: float32 [2048], replicated
- grad_gate: float32 [2048, 5632], P('dp', 'tensor')
- grad_up: float32 [2048, 5632], P('dp', 'tensor')
- grad_down: float32 [2048, 5632], P('dp', 'tensor')
Inputs may be any that keep to these rules, and one draw needn't show every extreme that they name: `lengths`: each sequence's valid tokens start at its slot's first position; in every draw some sequence fills its whole slot of 1024 positions.
All inputs are finite; a program needn't handle non-finite values.
Results may differ from a plain program's by a relative error of at most 0.025.
Values may be sent and summed in bfloat16 or wider, within the bound.
A program may use at most 320 MiB of HBM per device.

v0:
```python
import jax
import jax.numpy as jnp
from jax import lax
from jax.sharding import PartitionSpec as P

BLOCK = 64


def plain_dot(left_mat, right_mat):
    return jnp.dot(left_mat, right_mat, preferred_element_type=jnp.float32)


def dot_rows(left_mat, right_mat):
    return lax.dot_general(
        left_mat, right_mat, (((1,), (1,)), ((), ())), preferred_element_type=jnp.float32
    )


def dot_tokens(left_mat, right_mat):
    return lax.dot_general(
        left_mat, right_mat, (((0,), (0,)), ((), ())), preferred_element_type=jnp.float32
    )


def rms_apply(values, gain_vec):
    return values * lax.rsqrt(jnp.mean(values * values, axis=-1, keepdims=True) + 1e-05) * gain_vec


def unit_rows(values):
    return values * lax.rsqrt(jnp.sum(values * values, axis=-1, keepdims=True) + 1e-06)


def swiglu(gate_pre, up_pre):
    return jax.nn.silu(gate_pre) * up_pre


def short_conv(values, weight):
    tap_count = weight.shape[2]
    row_count = values.shape[0]
    tap_table = jnp.transpose(weight, (1, 0, 2)).reshape(-1, tap_count)
    padded = jnp.pad(values, ((tap_count - 1, 0), (0, 0)))
    summed = padded[0:row_count] * tap_table[:, 0]
    for tap_index in range(1, tap_count):
        summed = summed + padded[tap_index : tap_index + row_count] * tap_table[:, tap_index]
    return jax.nn.silu(summed)


def block_step(carry_state, pieces):
    query_rows, key_rows, value_rows, beta_rows, decay_rows = pieces
    running = jnp.cumsum(decay_rows, axis=0)
    query_h = jnp.transpose(query_rows, (1, 0, 2))
    key_h = jnp.transpose(key_rows, (1, 0, 2))
    value_h = jnp.transpose(value_rows, (1, 0, 2))
    beta_h = jnp.transpose(beta_rows)
    cum_h = jnp.transpose(running)
    size_c = query_rows.shape[0]
    pos_row = lax.broadcasted_iota(jnp.int32, (size_c, size_c), 0)
    pos_col = lax.broadcasted_iota(jnp.int32, (size_c, size_c), 1)
    lower_inc = pos_row >= pos_col
    lower_strict = pos_row > pos_col
    differ = cum_h[:, :, None] - cum_h[:, None, :]
    within = jnp.where(lower_inc, jnp.exp(jnp.where(lower_inc, differ, 0.0)), 0.0)
    key_key = jnp.einsum("htd,hjd->htj", key_h, key_h, preferred_element_type=jnp.float32)
    coupling = jnp.where(lower_strict, beta_h[:, :, None] * within * key_key, 0.0)
    start_decay = jnp.exp(cum_h)
    key_state = jnp.einsum("htd,hde->hte", key_h, carry_state, preferred_element_type=jnp.float32)
    right_side = beta_h[:, :, None] * value_h - (beta_h * start_decay)[:, :, None] * key_state
    identity_mat = jnp.eye(size_c, dtype=jnp.float32)
    new_values = jax.scipy.linalg.solve_triangular(
        identity_mat + coupling, right_side, lower=True, unit_diagonal=True
    )
    query_key = jnp.einsum("htd,hjd->htj", query_h, key_h, preferred_element_type=jnp.float32)
    query_state = jnp.einsum(
        "htd,hde->hte", query_h, carry_state, preferred_element_type=jnp.float32
    )
    output = start_decay[:, :, None] * query_state + jnp.einsum(
        "htj,hje->hte", query_key * within, new_values, preferred_element_type=jnp.float32
    )
    end_decay = cum_h[:, -1]
    tail_decay = jnp.exp(end_decay[:, None] - cum_h)
    carry_state = jnp.exp(end_decay)[:, None, None] * carry_state + jnp.einsum(
        "hjd,hje->hde",
        key_h * tail_decay[:, :, None],
        new_values,
        preferred_element_type=jnp.float32,
    )
    return (carry_state, jnp.transpose(output, (1, 0, 2)))


def delta_rule(query_rows, key_rows, value_rows, beta_rows, decay_rows):
    row_count, heads_n, key_size = query_rows.shape
    value_size = value_rows.shape[2]
    blocks = row_count // BLOCK

    def to_blocks(array_in):
        return array_in.reshape((blocks, BLOCK) + array_in.shape[1:])

    carry_state = jnp.zeros((heads_n, key_size, value_size), jnp.float32)
    unused, outputs = lax.scan(
        jax.checkpoint(block_step),
        carry_state,
        (
            to_blocks(query_rows),
            to_blocks(key_rows),
            to_blocks(value_rows),
            to_blocks(beta_rows),
            to_blocks(decay_rows),
        ),
    )
    return outputs.reshape(row_count, heads_n, value_size)


def mixer_core(
    q_raw, k_raw, v_raw, og_raw, b_raw, a_raw, conv_q, conv_k, conv_v, a_log, dt_bias, head_gain
):
    row_count = q_raw.shape[0]
    heads_n = a_log.shape[0]
    key_size = conv_q.shape[0]
    value_size = conv_v.shape[0]
    query_rows = unit_rows(
        short_conv(q_raw, conv_q).reshape(row_count, heads_n, key_size)
    ) * key_size ** (-0.5)
    key_rows = unit_rows(short_conv(k_raw, conv_k).reshape(row_count, heads_n, key_size))
    value_rows = short_conv(v_raw, conv_v).reshape(row_count, heads_n, value_size)
    beta_rows = jax.nn.sigmoid(b_raw)
    decay_rows = -jnp.exp(a_log) * jax.nn.softplus(a_raw + dt_bias)
    delta_out = delta_rule(query_rows, key_rows, value_rows, beta_rows, decay_rows)
    normed = rms_apply(delta_out, head_gain) * jax.nn.silu(
        og_raw.reshape(row_count, heads_n, value_size)
    )
    return normed.reshape(row_count, heads_n * value_size)


def shards(
    inputs,
    cotangent,
    lengths,
    norm1_gain,
    w_query,
    w_key,
    w_value,
    w_outgate,
    w_beta,
    w_alpha,
    conv_query,
    conv_key,
    conv_value,
    a_log,
    dt_bias,
    head_gain,
    w_out,
    norm2_gain,
    w_gate,
    w_up,
    w_down,
):
    local_rows = inputs[0].astype(jnp.float32)
    row_count = local_rows.shape[0]
    tensor_pos = lax.axis_index("tensor")
    positions = tensor_pos * row_count + jnp.arange(row_count, dtype=jnp.int32)
    valid_rows = (positions < lengths[0]).astype(jnp.float32)[:, None]
    (
        full_query,
        full_key,
        full_value,
        full_outgate,
        full_beta,
        full_alpha,
        full_out,
        full_gate,
        full_up,
        full_down,
        whole_convq,
        whole_convk,
        whole_convv,
    ) = (
        lax.all_gather(w_query, "dp", axis=0, tiled=True),
        lax.all_gather(w_key, "dp", axis=0, tiled=True),
        lax.all_gather(w_value, "dp", axis=0, tiled=True),
        lax.all_gather(w_outgate, "dp", axis=0, tiled=True),
        lax.all_gather(w_beta, "dp", axis=0, tiled=True),
        lax.all_gather(w_alpha, "dp", axis=0, tiled=True),
        lax.all_gather(w_out, "dp", axis=0, tiled=True),
        lax.all_gather(w_gate, "dp", axis=0, tiled=True),
        lax.all_gather(w_up, "dp", axis=0, tiled=True),
        lax.all_gather(w_down, "dp", axis=0, tiled=True),
        lax.all_gather(conv_query, "dp", axis=0, tiled=True),
        lax.all_gather(conv_key, "dp", axis=0, tiled=True),
        lax.all_gather(conv_value, "dp", axis=0, tiled=True),
    )
    heads_local = w_beta.shape[1]
    head_start = tensor_pos * heads_local
    alog_local = lax.dynamic_slice_in_dim(a_log, head_start, heads_local)
    dtb_local = lax.dynamic_slice_in_dim(dt_bias, head_start, heads_local)
    normed_one, norm_one_back = jax.vjp(rms_apply, local_rows, norm1_gain)
    rows_one = lax.all_gather(normed_one.astype(jnp.bfloat16), "tensor", axis=0, tiled=True)
    q_raw = plain_dot(rows_one, full_query)
    k_raw = plain_dot(rows_one, full_key)
    v_raw = plain_dot(rows_one, full_value)
    og_raw = plain_dot(rows_one, full_outgate)
    b_raw = plain_dot(rows_one, full_beta)
    a_raw = plain_dot(rows_one, full_alpha)
    head_out, core_back = jax.vjp(
        mixer_core,
        q_raw,
        k_raw,
        v_raw,
        og_raw,
        b_raw,
        a_raw,
        whole_convq.astype(jnp.float32),
        whole_convk.astype(jnp.float32),
        whole_convv.astype(jnp.float32),
        alog_local,
        dtb_local,
        head_gain,
    )
    head_bf = head_out.astype(jnp.bfloat16)
    part_rows = head_bf
    mixed_rows = lax.psum_scatter(
        dot_rows(part_rows, full_out), "tensor", scatter_dimension=0, tiled=True
    )
    after_mix = local_rows + mixed_rows
    normed_two, norm_two_back = jax.vjp(rms_apply, after_mix, norm2_gain)
    rows_two = lax.all_gather(normed_two.astype(jnp.bfloat16), "tensor", axis=0, tiled=True)
    gate_pre = plain_dot(rows_two, full_gate)
    up_pre = plain_dot(rows_two, full_up)
    hidden, swiglu_back = jax.vjp(swiglu, gate_pre, up_pre)
    hidden_bf = hidden.astype(jnp.bfloat16)
    part_rows = hidden_bf
    ffn_part = lax.psum_scatter(
        dot_rows(part_rows, full_down).astype(jnp.bfloat16),
        "tensor",
        scatter_dimension=0,
        tiled=True,
    ).astype(jnp.float32)
    after_ffn = after_mix + ffn_part
    outputs = (after_ffn * valid_rows).astype(jnp.bfloat16)[None]
    (
        back_query,
        back_key,
        back_value,
        back_outgate,
        back_beta,
        back_alpha,
        back_out,
        back_gate,
        back_up,
        back_down,
    ) = (
        lax.all_gather(w_query, "dp", axis=0, tiled=True),
        lax.all_gather(w_key, "dp", axis=0, tiled=True),
        lax.all_gather(w_value, "dp", axis=0, tiled=True),
        lax.all_gather(w_outgate, "dp", axis=0, tiled=True),
        lax.all_gather(w_beta, "dp", axis=0, tiled=True),
        lax.all_gather(w_alpha, "dp", axis=0, tiled=True),
        lax.all_gather(w_out, "dp", axis=0, tiled=True),
        lax.all_gather(w_gate, "dp", axis=0, tiled=True),
        lax.all_gather(w_up, "dp", axis=0, tiled=True),
        lax.all_gather(w_down, "dp", axis=0, tiled=True),
    )
    grad_after = valid_rows * cotangent[0].astype(jnp.float32)
    grad_ffn = grad_after.astype(jnp.bfloat16)
    incoming = lax.all_gather(grad_ffn, "tensor", axis=0, tiled=True)
    grad_hidden = plain_dot(incoming, back_down)
    grad_down_w = dot_tokens(incoming, hidden_bf)
    grad_hidden, grad_down_w = (grad_hidden, grad_down_w)
    grad_gate_pre, grad_up_pre = swiglu_back(grad_hidden)
    gate_low = grad_gate_pre.astype(jnp.bfloat16)
    up_low = grad_up_pre.astype(jnp.bfloat16)
    grad_gate_w = dot_tokens(rows_two, gate_low)
    grad_up_w = dot_tokens(rows_two, up_low)
    grad_normed_two = lax.psum_scatter(
        dot_rows(gate_low, back_gate) + dot_rows(up_low, back_up),
        "tensor",
        scatter_dimension=0,
        tiled=True,
    )
    grad_mid, grad_norm2 = norm_two_back(grad_normed_two)
    grad_mid = grad_mid + grad_after
    grad_mix = grad_mid.astype(jnp.bfloat16)
    incoming = lax.all_gather(grad_mix, "tensor", axis=0, tiled=True)
    grad_head = plain_dot(incoming, back_out)
    grad_out_w = dot_tokens(incoming, head_bf)
    grad_head, grad_out_w = (grad_head, grad_out_w)
    (
        grad_q_f,
        grad_k_f,
        grad_v_f,
        grad_og_f,
        grad_b_f,
        grad_a_f,
        grad_cq,
        grad_ck,
        grad_cv,
        grad_alog_local,
        grad_dtb_local,
        grad_head_gain,
    ) = core_back(grad_head)
    grad_q_low = grad_q_f.astype(jnp.bfloat16)
    grad_k_low = grad_k_f.astype(jnp.bfloat16)
    grad_v_low = grad_v_f.astype(jnp.bfloat16)
    grad_og_low = grad_og_f.astype(jnp.bfloat16)
    grad_b_low = grad_b_f.astype(jnp.bfloat16)
    grad_a_low = grad_a_f.astype(jnp.bfloat16)
    grad_query_w = dot_tokens(rows_one, grad_q_low)
    grad_key_w = dot_tokens(rows_one, grad_k_low)
    grad_value_w = dot_tokens(rows_one, grad_v_low)
    grad_outgate_w = dot_tokens(rows_one, grad_og_low)
    grad_beta_w = dot_tokens(rows_one, grad_b_low)
    grad_alpha_w = dot_tokens(rows_one, grad_a_low)
    summed = dot_rows(grad_q_low, back_query) + dot_rows(grad_k_low, back_key)
    summed = summed + dot_rows(grad_v_low, back_value) + dot_rows(grad_og_low, back_outgate)
    grad_normed_one = lax.psum_scatter(
        (summed + dot_rows(grad_b_low, back_beta) + dot_rows(grad_a_low, back_alpha)).astype(
            jnp.bfloat16
        ),
        "tensor",
        scatter_dimension=0,
        tiled=True,
    ).astype(jnp.float32)
    grad_first, grad_norm1 = norm_one_back(grad_normed_one)
    grad_inputs = (grad_mid + grad_first)[None]
    all_shards = (
        lax.psum_scatter(
            grad_query_w.astype(jnp.bfloat16), "dp", scatter_dimension=0, tiled=True
        ).astype(jnp.float32),
        lax.psum_scatter(
            grad_key_w.astype(jnp.bfloat16), "dp", scatter_dimension=0, tiled=True
        ).astype(jnp.float32),
        lax.psum_scatter(
            grad_value_w.astype(jnp.bfloat16), "dp", scatter_dimension=0, tiled=True
        ).astype(jnp.float32),
        lax.psum_scatter(
            grad_outgate_w.astype(jnp.bfloat16), "dp", scatter_dimension=0, tiled=True
        ).astype(jnp.float32),
        lax.psum_scatter(
            grad_beta_w.astype(jnp.bfloat16), "dp", scatter_dimension=0, tiled=True
        ).astype(jnp.float32),
        lax.psum_scatter(
            grad_alpha_w.astype(jnp.bfloat16), "dp", scatter_dimension=0, tiled=True
        ).astype(jnp.float32),
        lax.psum_scatter(
            grad_out_w.astype(jnp.bfloat16), "dp", scatter_dimension=0, tiled=True
        ).astype(jnp.float32),
        lax.psum_scatter(
            grad_cq.astype(jnp.bfloat16), "dp", scatter_dimension=0, tiled=True
        ).astype(jnp.float32),
        lax.psum_scatter(
            grad_ck.astype(jnp.bfloat16), "dp", scatter_dimension=0, tiled=True
        ).astype(jnp.float32),
        lax.psum_scatter(
            grad_cv.astype(jnp.bfloat16), "dp", scatter_dimension=0, tiled=True
        ).astype(jnp.float32),
        lax.psum_scatter(
            grad_gate_w.astype(jnp.bfloat16), "dp", scatter_dimension=0, tiled=True
        ).astype(jnp.float32),
        lax.psum_scatter(
            grad_up_w.astype(jnp.bfloat16), "dp", scatter_dimension=0, tiled=True
        ).astype(jnp.float32),
        lax.psum_scatter(
            grad_down_w.astype(jnp.bfloat16), "dp", scatter_dimension=0, tiled=True
        ).astype(jnp.float32),
    )
    alog_full = lax.dynamic_update_slice_in_dim(
        jnp.zeros_like(a_log), grad_alog_local, head_start, 0
    )
    dtb_full = lax.dynamic_update_slice_in_dim(
        jnp.zeros_like(dt_bias), grad_dtb_local, head_start, 0
    )
    small_sums = lax.psum(
        (grad_norm1, grad_norm2, grad_head_gain, alog_full, dtb_full), ("dp", "tensor")
    )
    return (
        outputs,
        grad_inputs,
        small_sums[0],
        all_shards[0],
        all_shards[1],
        all_shards[2],
        all_shards[3],
        all_shards[4],
        all_shards[5],
        all_shards[7],
        all_shards[8],
        all_shards[9],
        small_sums[3],
        small_sums[4],
        small_sums[2],
        all_shards[6],
        small_sums[1],
        all_shards[10],
        all_shards[11],
        all_shards[12],
    )


def solution(mesh):
    in_specs = (
        P("dp", "tensor", None),
        P("dp", "tensor", None),
        P("dp"),
        P(),
        P("dp", "tensor"),
        P("dp", "tensor"),
        P("dp", "tensor"),
        P("dp", "tensor"),
        P("dp", "tensor"),
        P("dp", "tensor"),
        P("dp", "tensor", None),
        P("dp", "tensor", None),
        P("dp", "tensor", None),
        P(),
        P(),
        P(),
        P("dp", "tensor"),
        P(),
        P("dp", "tensor"),
        P("dp", "tensor"),
        P("dp", "tensor"),
    )
    out_specs = (
        P("dp", "tensor", None),
        P("dp", "tensor", None),
        P(),
        P("dp", "tensor"),
        P("dp", "tensor"),
        P("dp", "tensor"),
        P("dp", "tensor"),
        P("dp", "tensor"),
        P("dp", "tensor"),
        P("dp", "tensor", None),
        P("dp", "tensor", None),
        P("dp", "tensor", None),
        P(),
        P(),
        P(),
        P("dp", "tensor"),
        P(),
        P("dp", "tensor"),
        P("dp", "tensor"),
        P("dp", "tensor"),
    )
    return jax.shard_map(shards, mesh=mesh, in_specs=in_specs, out_specs=out_specs, check_vma=False)
```

profile of v0, /device:TPU:0, one launch (start us, length us, event | category | flops | bytes accessed | tf_op | source)
XLA Modules:
  0.0 2830.2 jit_solution(6911755327145607036)
XLA Ops:
  16.0 32.8 %all_gather.64 = bf16[128,4,4]{2,1,0:T(4,128)(2,1)S(1)} all-gather(bf16[16,4,4]{2,1,0:T(4,128)(2,1)S(1)} %copy.363), channel_id=1, replica_groups=mesh['dp'=8,'tensor'=4] {'dp'}, dimensions={0}, use_global_device_ids=true | all-gather | bytes 4608 | tf_op jit(solution)/shard_map/all_gather | solution.py:188
  49.2 30.7 %all_gather.69 = bf16[128,4,4]{2,1,0:T(4,128)(2,1)S(1)} all-gather(bf16[16,4,4]{2,1,0:T(4,128)(2,1)S(1)} %copy.370), channel_id=1, replica_groups=mesh['dp'=8,'tensor'=4] {'dp'}, dimensions={0}, use_global_device_ids=true | all-gather | bytes 4608 | tf_op jit(solution)/shard_map/all_gather | solution.py:187
  80.2 26.0 all_gather.62
  106.4 31.3 %all_gather.67 = bf16[256,4,4]{2,1,0:T(4,128)(2,1)S(1)} all-gather(bf16[32,4,4]{2,1,0:T(4,128)(2,1)S(1)} %copy.368), channel_id=1, replica_groups=mesh['dp'=8,'tensor'=4] {'dp'}, dimensions={0}, use_global_device_ids=true | all-gather | bytes 9216 | tf_op jit(solution)/shard_map/all_gather | solution.py:189
  138.0 26.2 all_gather.65
  248.2 475.4 %while.44 = (s32[]{:T(128)}, f32[4,128,256]{2,1,0:T(8,128)S(1)}, f32[16,64,4,256]{3,1,2,0:T(8,128)}, f32[16,4,128,256]{3,2,1,0:T(8,128)}, f32[16,64,4]{2,1,0:T(8...) while((s32[]{:T(128)}, f32[4,128,256]{2,1,0:T(8,128)S(1)}, ...), condition=%wide.region_5.7_spmd.clone.clone, body=%wide.region_3.6_spmd.clone.clone.sunk | while | flops 118853952 | bytes 5871870 | solution.py:99
  763.6 69.3 %reduce-scatter.28.cloned.1.call-done = f32[256,2048]{1,0:T(8,128)} async-done(((f32[1024,2048]{1,0:T(8,128)}), f32[256,2048]{1,0:T(8,128)}) %reduce-scatter.28.cloned.1.call-update) | async-done | bytes 2097168 | tf_op jit(solution)/shard_map/reduce_scatter | solution.py:220
  839.3 88.7 %all-gather.27.cloned.1.call-done = bf16[2048,1408]{1,0:T(8,128)(2,1)} async-done(((bf16[256,1408]{1,0:T(8,128)(2,1)}), bf16[2048,1408]{1,0:T(8,128)(2,1)}) %all-gather.27.cloned.1.call-update) | async-done | bytes 5767184 | tf_op jit(solution)/shard_map/all_gather | solution.py:184
  928.0 34.9 %all-gather.25.cloned.1.call-done = bf16[1024,2048]{1,0:T(8,128)(2,1)} async-done(((bf16[256,2048]{1,0:T(8,128)(2,1)}), bf16[1024,2048]{1,0:T(8,128)(2,1)}) %all-gather.25.cloned.1.call-update) | async-done | bytes 4194320 | tf_op jit(solution)/shard_map/all_gather | solution.py:225
  974.7 83.1 %all-gather.29.cloned.1.call-done = bf16[2048,1408]{1,0:T(8,128)(2,1)} async-done(((bf16[256,1408]{1,0:T(8,128)(2,1)}), bf16[2048,1408]{1,0:T(8,128)(2,1)}) %all-gather.29.cloned.1.call-update) | async-done | bytes 5767184 | tf_op jit(solution)/shard_map/all_gather | solution.py:185
  1092.7 95.0 %all-gather.31.cloned.1.call-done = bf16[2048,1408]{1,0:T(8,128)(2,1)} async-done(((bf16[256,1408]{1,0:T(8,128)(2,1)}), bf16[2048,1408]{1,0:T(8,128)(2,1)}) %all-gather.31.cloned.1.call-update) | async-done | bytes 5767184 | tf_op jit(solution)/shard_map/all_gather | solution.py:186
  1234.4 58.7 %reduce-scatter.32.cloned.1.call-done = f32[256,2048]{1,0:T(8,128)} async-done(((f32[1024,2048]{1,0:T(8,128)}), f32[256,2048]{1,0:T(8,128)}) %reduce-scatter.32.cloned.1.call-update) | async-done | bytes 2097168 | tf_op jit(solution)/shard_map/reduce_scatter | solution.py:273
  1295.9 44.2 %reduce-scatter.30.cloned.1.call-done = bf16[256,2048]{1,0:T(8,128)(2,1)} async-done(((bf16[1024,2048]{1,0:T(8,128)(2,1)}), bf16[256,2048]{1,0:T(8,128)(2,1)}) %reduce-scatter.30.cloned.1.call-update) | async-done | bytes 1048592 | tf_op jit(solution)/shard_map/reduce_scatter | solution.py:231
  1427.2 588.8 %while.43 = (s32[]{:T(128)}, f32[4,128,256]{2,1,0:T(8,128)S(1)}, f32[16,64,4,128]{3,1,2,0:T(8,128)}, f32[16,64,4,128]{3,1,2,0:T(8,128)}, f32[16,64,4,256]{3,2,1,...) while((s32[]{:T(128)}, f32[4,128,256]{2,1,0:T(8,128)S(1)}, ...), condition=%wide.region_25.27_spmd.clone, body=%wide.region_13.26_spmd.clone.sunk | while | flops 342849856 | bytes 21298192 | solution.py:99
  2182.9 42.1 %reduce-scatter.60.cloned.1.call-done = bf16[32,16]{1,0:T(8,128)(2,1)} async-done(((bf16[256,16]{1,0:T(8,128)(2,1)}), bf16[32,16]{1,0:T(8,128)(2,1)}) %reduce-scatter.60.cloned.1.call-update) | async-done | bytes 1040
  2226.4 63.9 %reduce-scatter.54.cloned.1.call-done = bf16[256,4]{1,0:T(8,128)(2,1)} async-done(((bf16[2048,4]{1,0:T(8,128)(2,1)}), bf16[256,4]{1,0:T(8,128)(2,1)}) %reduce-scatter.54.cloned.1.call-update) | async-done | bytes 2064
  2291.8 63.3 %reduce-scatter.52.cloned.1.call-done = bf16[256,4]{1,0:T(8,128)(2,1)} async-done(((bf16[2048,4]{1,0:T(8,128)(2,1)}), bf16[256,4]{1,0:T(8,128)(2,1)}) %reduce-scatter.52.cloned.1.call-update) | async-done | bytes 2064
  2356.6 69.0 %reduce-scatter.38.cloned.1.call-done = bf16[256,512]{1,0:T(8,128)(2,1)} async-done(((bf16[2048,512]{1,0:T(8,128)(2,1)}), bf16[256,512]{1,0:T(8,128)(2,1)}) %reduce-scatter.38.cloned.1.call-update) | async-done | bytes 262160 | tf_op jit(solution)/shard_map/reduce_scatter | solution.py:328
  2427.5 68.9 %reduce-scatter.36.cloned.1.call-done = bf16[256,512]{1,0:T(8,128)(2,1)} async-done(((bf16[2048,512]{1,0:T(8,128)(2,1)}), bf16[256,512]{1,0:T(8,128)(2,1)}) %reduce-scatter.36.cloned.1.call-update) | async-done | bytes 262160 | tf_op jit(solution)/shard_map/reduce_scatter | solution.py:325
  2498.2 89.0 %reduce-scatter.44.cloned.1.call-done = bf16[256,1024]{1,0:T(8,128)(2,1)} async-done(((bf16[2048,1024]{1,0:T(8,128)(2,1)}), bf16[256,1024]{1,0:T(8,128)(2,1)}) %reduce-scatter.44.cloned.1.call-update) | async-done | bytes 524304 | tf_op jit(solution)/shard_map/reduce_scatter | solution.py:343
  2589.3 89.0 %reduce-scatter.40.cloned.1.call-done = bf16[256,1024]{1,0:T(8,128)(2,1)} async-done(((bf16[2048,1024]{1,0:T(8,128)(2,1)}), bf16[256,1024]{1,0:T(8,128)(2,1)}) %reduce-scatter.40.cloned.1.call-update) | async-done | bytes 524304 | tf_op jit(solution)/shard_map/reduce_scatter | solution.py:331
  2680.5 44.9 %reduce-scatter.34.cloned.1.call-done = bf16[256,2048]{1,0:T(8,128)(2,1)} async-done(((bf16[1024,2048]{1,0:T(8,128)(2,1)}), bf16[256,2048]{1,0:T(8,128)(2,1)}) %reduce-scatter.34.cloned.1.call-update) | async-done | bytes 1048592 | tf_op jit(solution)/shard_map/reduce_scatter | solution.py:314
  2727.6 42.2 %all-reduce.28 = (f32[2048]{0:T(1024)}, f32[16]{0:T(128)}, f32[16]{0:T(128)}, f32[256]{0:T(256)}, f32[2048]{0:T(1024)}) all-reduce(f32[2048]{0:T(1024)S(1)} %get-tuple-element.756, f32[16]{0:T(128)S(1)} %multiply_dynamic-update-slice_fusion, f32[16]{0:T(128)S(1)} %dynamic_update_slice.68, ...), channel_id=1, replica_groups=mesh['dp'=8,'tensor'=4] {'dp','tensor'}, use_global_device_ids=true, to_apply=%region_31.33 | all-reduce | flops 4384 | bytes 35072 | tf_op jit(solution)/shard_map/psum | solution.py:371
  2769.9 48.3 %reduce-scatter.42.cloned.1.call-done = bf16[256,1024]{1,0:T(8,128)(2,1)} async-done(((bf16[2048,1024]{1,0:T(8,128)(2,1)}), bf16[256,1024]{1,0:T(8,128)(2,1)}) %reduce-scatter.42.cloned.1.call-update) | async-done | bytes 524304 | tf_op jit(solution)/shard_map/reduce_scatter | solution.py:334
  (1662 shorter events, 1568.2 us)
Async XLA Ops:
  13.3 164.3 %all-gather.19.cloned.1.call-start = ((), (), s32[]{:S(2)}) async-start(), calls=%async_computation.20 | async-start | bytes 2359296 | tf_op jit(solution)/shard_map/all_gather | solution.py:177
  14.0 211.3 %all-gather.17.cloned.1.call-start = ((), (), s32[]{:S(2)}) async-start(), calls=%async_computation.19 | async-start | bytes 4718592 | tf_op jit(solution)/shard_map/all_gather | solution.py:179
  14.6 725.6 %all-gather.21.cloned.1.call-start = ((), (), s32[]{:S(2)}) async-start(), calls=%async_computation.21 | async-start | bytes 4718592 | tf_op jit(solution)/shard_map/all_gather | solution.py:180
  15.2 737.8 %all-gather.23.cloned.1.call-start = ((), (), s32[]{:S(2)}) async-start(), calls=%async_computation.22 | async-start | bytes 4718592 | tf_op jit(solution)/shard_map/all_gather | solution.py:183
  15.8 817.1 %reduce-scatter.28.cloned.1.call-start = ((), (), s32[]{:S(2)}) async-start(), calls=%async_computation.23 | async-start | bytes 10485760 | tf_op jit(solution)/shard_map/reduce_scatter | solution.py:220
  762.8 165.2 %all-gather.27.cloned.1.call-start = ((), (), s32[]{:S(2)}) async-start(), calls=%async_computation.25 | async-start | bytes 6488064 | tf_op jit(solution)/shard_map/all_gather | solution.py:184
  763.5 199.3 %all-gather.25.cloned.1.call-start = ((), (), s32[]{:S(2)}) async-start(), calls=%async_computation.24 | async-start | bytes 5242880 | tf_op jit(solution)/shard_map/all_gather | solution.py:225
  836.1 221.7 %all-gather.29.cloned.1.call-start = ((), (), s32[]{:S(2)}) async-start(), calls=%async_computation.26 | async-start | bytes 6488064 | tf_op jit(solution)/shard_map/all_gather | solution.py:185
  836.7 256.1 %all-gather.33.cloned.1.call-start = ((), (), s32[]{:S(2)}) async-start(), calls=%async_computation.29 | async-start | bytes 5242880 | tf_op jit(solution)/shard_map/all_gather | solution.py:264
  838.6 349.1 %all-gather.31.cloned.1.call-start = ((), (), s32[]{:S(2)}) async-start(), calls=%async_computation.27 | async-start | bytes 6488064 | tf_op jit(solution)/shard_map/all_gather | solution.py:186
  839.2 454.0 %reduce-scatter.32.cloned.1.call-start = ((), (), s32[]{:S(2)}) async-start(), calls=%async_computation.30 | async-start | bytes 10485760 | tf_op jit(solution)/shard_map/reduce_scatter | solution.py:273
  1344.9 827.9 %reduce-scatter.46.cloned.1.call-start = ((), (), s32[]{:S(2)}) async-start(), calls=%async_computation.38 | async-start | bytes 6488064 | tf_op jit(solution)/shard_map/reduce_scatter | solution.py:355
  1356.0 819.2 %reduce-scatter.48.cloned.1.call-start = ((), (), s32[]{:S(2)}) async-start(), calls=%async_computation.39 | async-start | bytes 6488064 | tf_op jit(solution)/shard_map/reduce_scatter | solution.py:358
  1368.7 808.7 %reduce-scatter.50.cloned.1.call-start = ((), (), s32[]{:S(2)}) async-start(), calls=%async_computation.40 | async-start | bytes 6488064 | tf_op jit(solution)/shard_map/reduce_scatter | solution.py:361
  1387.5 792.6 %reduce-scatter.58.cloned.1.call-start = ((), (), s32[]{:S(2)}) async-start(), calls=%async_computation.44 | async-start | bytes 36864
  2058.8 166.2 %reduce-scatter.60.cloned.1.call-start = ((), (), s32[]{:S(2)}) async-start(), calls=%async_computation.45 | async-start | bytes 73728
  2060.1 230.2 %reduce-scatter.54.cloned.1.call-start = ((), (), s32[]{:S(2)}) async-start(), calls=%async_computation.42 | async-start | bytes 589824
  2064.3 290.8 %reduce-scatter.52.cloned.1.call-start = ((), (), s32[]{:S(2)}) async-start(), calls=%async_computation.41 | async-start | bytes 589824
  2068.4 357.3 %reduce-scatter.38.cloned.1.call-start = ((), (), s32[]{:S(2)}) async-start(), calls=%async_computation.34 | async-start | bytes 2359296 | tf_op jit(solution)/shard_map/reduce_scatter | solution.py:328
  2076.5 419.8 %reduce-scatter.36.cloned.1.call-start = ((), (), s32[]{:S(2)}) async-start(), calls=%async_computation.33 | async-start | bytes 2359296 | tf_op jit(solution)/shard_map/reduce_scatter | solution.py:325
  2085.5 501.7 %reduce-scatter.44.cloned.1.call-start = ((), (), s32[]{:S(2)}) async-start(), calls=%async_computation.37 | async-start | bytes 4718592 | tf_op jit(solution)/shard_map/reduce_scatter | solution.py:343
  2094.2 584.2 %reduce-scatter.40.cloned.1.call-start = ((), (), s32[]{:S(2)}) async-start(), calls=%async_computation.35 | async-start | bytes 4718592 | tf_op jit(solution)/shard_map/reduce_scatter | solution.py:331
  2117.5 607.8 %reduce-scatter.34.cloned.1.call-start = ((), (), s32[]{:S(2)}) async-start(), calls=%async_computation.32 | async-start | bytes 5242880 | tf_op jit(solution)/shard_map/reduce_scatter | solution.py:314
  2164.1 654.0 %reduce-scatter.42.cloned.1.call-start = ((), (), s32[]{:S(2)}) async-start(), calls=%async_computation.36 | async-start | bytes 4718592 | tf_op jit(solution)/shard_map/reduce_scatter | solution.py:334
  (116 other events, 6157.2 us)
Sparse Core Ops, SparseCore 0:
  10.1 53.4 all-gather.14
  101.0 49.7 all-gather.18
  152.8 72.5 all-gather.16
  227.3 72.1 all-gather.20
  301.4 72.1 all-gather.22
  762.9 69.9 reduce-scatter.27
  835.3 92.6 all-gather.26
  965.1 92.6 all-gather.28
  1095.0 92.6 all-gather.30
  1223.2 69.9 reduce-scatter.31
  1295.6 44.4 reduce-scatter.29
  1383.5 110.0 reduce-scatter.45
  1497.5 109.5 reduce-scatter.47
  1611.0 110.0 reduce-scatter.49
  2050.8 53.6 reduce-scatter.57
  2107.8 52.5 reduce-scatter.55
  2164.7 60.2 reduce-scatter.59
  2229.3 60.9 reduce-scatter.53
  2294.2 60.8 reduce-scatter.51
  2358.9 66.7 reduce-scatter.37
  2429.6 66.6 reduce-scatter.35
  2500.3 86.8 reduce-scatter.43
  2590.7 87.6 reduce-scatter.39
  2729.0 89.1 reduce-scatter.41
  (5 shorter events, 176.8 us)
where the time goes:
time: 2840 us; the launch traced here: 2830 us
  waiting for transfers between devices  1100 us (39%)
  other arithmetic  805 us (28%)
  matrix products  475 us (17%)
  local copies, waits for them, and re-layouts  241 us (8%)
  blocking collectives  189 us (7%)
    another operation x128, other arithmetic, block_step(): jax.scipy.linalg.solve_triangular(identity_mat + coupling, right_side, lo...  634 us
    unnamed x34, waiting for transfers between devices  174 us
    squeeze x112, local copies, waits for them, and re-layouts, delta_rule(): lax.scan(jax.checkpoint(block_step), carry_state, (to_blocks(query_rows),...  98.1 us
    all_gather x1, waiting for transfers between devices, shards(): lax.all_gather(w_down, 'dp', axis=0, tiled=True)  95 us
    dot_general x10, matrix products, plain_dot(): return jnp.dot(left_mat, right_mat, preferred_element_type=jnp.float32)  90.6 us
    reduce_scatter x1, waiting for transfers between devices, shards(): lax.psum_scatter(grad_out_w.astype(jnp.bfloat16), 'dp', scatter_dimension...  89 us
    reduce_scatter x1, waiting for transfers between devices, shards(): lax.psum_scatter(grad_value_w.astype(jnp.bfloat16), 'dp', scatter_dimensi...  89 us
    all_gather x1, waiting for transfers between devices, shards(): lax.all_gather(w_gate, 'dp', axis=0, tiled=True)  88.7 us
  transfers between devices with their start and end apart: 29, of which 18 were waited for; matrix products, arithmetic and copies ran while one was open for 51% of the time, Pallas kernels for 0%

commit v1 on v0

--- a/solution.py
+++ b/solution.py
@@ -4,6 +4,17 @@
 from jax.sharding import PartitionSpec as P
 
 BLOCK = 64
+
+
+def ring_gather(x, axis, dim):
+    ways = lax.axis_size(axis)
+    pieces = [x]
+    for far in range(1, ways):
+        pieces.append(
+            lax.ppermute(pieces[far - 1], axis, [(d, (d - 1) % ways) for d in range(ways)])
+        )
+    line = jnp.concatenate(pieces, axis=dim)
+    return jnp.roll(line, lax.axis_index(axis) * x.shape[dim], axis=dim)
 
 
 def plain_dot(left_mat, right_mat):
@@ -181,7 +192,7 @@
         lax.all_gather(w_beta, "dp", axis=0, tiled=True),
         lax.all_gather(w_alpha, "dp", axis=0, tiled=True),
         lax.all_gather(w_out, "dp", axis=0, tiled=True),
-        lax.all_gather(w_gate, "dp", axis=0, tiled=True),
+        ring_gather(w_gate, "dp", 0),
         lax.all_gather(w_up, "dp", axis=0, tiled=True),
         lax.all_gather(w_down, "dp", axis=0, tiled=True),
         lax.all_gather(conv_query, "dp", axis=0, tiled=True),

time: 2840 us -> 2900 us (1.021)
  starting transfers between devices: 1.64 us -> 37.1 us
    ppermute x0 -> x7, waiting for transfers between devices: none -> 144 us  [ring_gather(): lax.ppermute(pieces[far - 1], axis, [(d, (d - 1) % ways) for d in range(w...]
    all_gather x1, waiting for transfers between devices: 95 us -> 0.01 us  [shards(): lax.all_gather(w_down, 'dp', axis=0, tiled=True)]
    ppermute x0 -> x7, starting transfers between devices: none -> 35.3 us  [ring_gather(): lax.ppermute(pieces[far - 1], axis, [(d, (d - 1) % ways) for d in range(w...]
    unnamed x245 -> x278, local copies, waits for them, and re-layouts: 40.9 us -> 62.6 us
  transfers between devices with their start and end apart: 29 -> 36, of which waited for: 18 -> 23; matrix products, arithmetic and copies ran while one was open for 51% -> 52% of each run, Pallas kernels for 0% -> 0%
where the time goes in v1:
time: 2900 us; the launch traced here: 2880 us
  waiting for transfers between devices  1090 us (38%)
  other arithmetic  808 us (28%)
  matrix products  474 us (16%)
  local copies, waits for them, and re-layouts  263 us (9%)
  blocking collectives  189 us (7%)
  starting transfers between devices  37.1 us (1%)
    another operation x128, other arithmetic, block_step(): jax.scipy.linalg.solve_triangular(identity_mat + coupling, right_side, lo...  634 us
    unnamed x34, waiting for transfers between devices  175 us
    ppermute x7, waiting for transfers between devices, ring_gather(): lax.ppermute(pieces[far - 1], axis, [(d, (d - 1) % ways) for d in range(w...  144 us
    squeeze x112, local copies, waits for them, and re-layouts, delta_rule(): lax.scan(jax.checkpoint(block_step), carry_state, (to_blocks(query_rows),...  98.1 us
    dot_general x10, matrix products, plain_dot(): return jnp.dot(left_mat, right_mat, preferred_element_type=jnp.float32)  90.4 us
    reduce_scatter x1, waiting for transfers between devices, shards(): lax.psum_scatter(grad_value_w.astype(jnp.bfloat16), 'dp', scatter_dimensi...  89.1 us
    reduce_scatter x1, waiting for transfers between devices, shards(): lax.psum_scatter(grad_out_w.astype(jnp.bfloat16), 'dp', scatter_dimension...  89 us
    dot_general x10, matrix products, dot_rows(): lax.dot_general(left_mat, right_mat, (((1,), (1,)), ((), ())), preferred_...  86 us
  transfers between devices with their start and end apart: 36, of which 23 were waited for; matrix products, arithmetic and copies ran while one was open for 52% of the time, Pallas kernels for 0%

profile of v1, /device:TPU:0, one launch (start us, length us, event | category | flops | bytes accessed | tf_op | source)
XLA Modules:
  0.0 2883.6 jit_solution(14716004856339613388)
XLA Ops:
  16.0 32.7 %all_gather.63 = bf16[128,4,4]{2,1,0:T(4,128)(2,1)S(1)} all-gather(bf16[16,4,4]{2,1,0:T(4,128)(2,1)S(1)} %copy.363), channel_id=1, replica_groups=mesh['dp'=8,'tensor'=4] {'dp'}, dimensions={0}, use_global_device_ids=true | all-gather | bytes 4608 | tf_op jit(solution)/shard_map/all_gather | solution.py:199
  49.1 30.6 %all_gather.68 = bf16[128,4,4]{2,1,0:T(4,128)(2,1)S(1)} all-gather(bf16[16,4,4]{2,1,0:T(4,128)(2,1)S(1)} %copy.370), channel_id=1, replica_groups=mesh['dp'=8,'tensor'=4] {'dp'}, dimensions={0}, use_global_device_ids=true | all-gather | bytes 4608 | tf_op jit(solution)/shard_map/all_gather | solution.py:198
  106.2 31.6 %all_gather.66 = bf16[256,4,4]{2,1,0:T(4,128)(2,1)S(1)} all-gather(bf16[32,4,4]{2,1,0:T(4,128)(2,1)S(1)} %copy.368), channel_id=1, replica_groups=mesh['dp'=8,'tensor'=4] {'dp'}, dimensions={0}, use_global_device_ids=true | all-gather | bytes 9216 | tf_op jit(solution)/shard_map/all_gather | solution.py:200
  138.1 26.1 all_gather.64
  248.4 475.4 %while.44 = (s32[]{:T(128)}, f32[4,128,256]{2,1,0:T(8,128)S(1)}, f32[16,64,4,256]{3,1,2,0:T(8,128)}, f32[16,4,128,256]{3,2,1,0:T(8,128)}, f32[16,64,4]{2,1,0:T(8...) while((s32[]{:T(128)}, f32[4,128,256]{2,1,0:T(8,128)S(1)}, ...), condition=%wide.region_5.7_spmd.clone.clone, body=%wide.region_3.6_spmd.clone.clone.sunk | while | flops 118853952 | bytes 5871870 | solution.py:110
  766.6 66.3 %reduce-scatter.28.cloned.1.call-done = f32[256,2048]{1,0:T(8,128)} async-done(((f32[1024,2048]{1,0:T(8,128)}), f32[256,2048]{1,0:T(8,128)}) %reduce-scatter.28.cloned.1.call-update) | async-done | bytes 2097168 | tf_op jit(solution)/shard_map/reduce_scatter | solution.py:231
  880.9 29.4 %collective-permute-done.2 = bf16[256,1408]{1,0:T(8,128)(2,1)S(1)} collective-permute-done((bf16[256,1408]{1,0:T(8,128)(2,1)S(1)}, bf16[256,1408]{1,0:T(8,128)(2,1)S(1)}, u32[]{:S(2)}, u32[]{:S(2)}) %collective-permute-start.2) | collective-permute-done | bytes 720928 | tf_op jit(solution)/shard_map/ppermute | solution.py:14
  940.8 27.6 collective-permute-done.4
  1051.7 72.9 %all-gather.27.cloned.1.call-done = bf16[2048,1408]{1,0:T(8,128)(2,1)} async-done(((bf16[256,1408]{1,0:T(8,128)(2,1)}), bf16[2048,1408]{1,0:T(8,128)(2,1)}) %all-gather.27.cloned.1.call-update) | async-done | bytes 5767184 | tf_op jit(solution)/shard_map/all_gather | solution.py:196
  1124.6 34.9 %all-gather.25.cloned.1.call-done = bf16[1024,2048]{1,0:T(8,128)(2,1)} async-done(((bf16[256,2048]{1,0:T(8,128)(2,1)}), bf16[1024,2048]{1,0:T(8,128)(2,1)}) %all-gather.25.cloned.1.call-update) | async-done | bytes 4194320 | tf_op jit(solution)/shard_map/all_gather | solution.py:236
  1186.2 68.3 %all-gather.33.cloned.1.call-done = bf16[2048,1408]{1,0:T(8,128)(2,1)} async-done(((bf16[256,1408]{1,0:T(8,128)(2,1)}), bf16[2048,1408]{1,0:T(8,128)(2,1)}) %all-gather.33.cloned.1.call-update) | async-done | bytes 5767184 | tf_op jit(solution)/shard_map/all_gather | solution.py:269
  1284.8 58.6 %reduce-scatter.32.cloned.1.call-done = f32[256,2048]{1,0:T(8,128)} async-done(((f32[1024,2048]{1,0:T(8,128)}), f32[256,2048]{1,0:T(8,128)}) %reduce-scatter.32.cloned.1.call-update) | async-done | bytes 2097168 | tf_op jit(solution)/shard_map/reduce_scatter | solution.py:284
  1346.1 44.2 %reduce-scatter.30.cloned.1.call-done = bf16[256,2048]{1,0:T(8,128)(2,1)} async-done(((bf16[1024,2048]{1,0:T(8,128)(2,1)}), bf16[256,2048]{1,0:T(8,128)(2,1)}) %reduce-scatter.30.cloned.1.call-update) | async-done | bytes 1048592 | tf_op jit(solution)/shard_map/reduce_scatter | solution.py:242
  1477.7 589.0 %while.43 = (s32[]{:T(128)}, f32[4,128,256]{2,1,0:T(8,128)S(1)}, f32[16,64,4,128]{3,1,2,0:T(8,128)}, f32[16,64,4,128]{3,1,2,0:T(8,128)}, f32[16,64,4,256]{3,2,1,...) while((s32[]{:T(128)}, f32[4,128,256]{2,1,0:T(8,128)S(1)}, ...), condition=%wide.region_25.27_spmd.clone, body=%wide.region_13.26_spmd.clone.sunk | while | flops 342849856 | bytes 21298192 | solution.py:110
  2234.6 43.6 %reduce-scatter.60.cloned.1.call-done = bf16[32,16]{1,0:T(8,128)(2,1)} async-done(((bf16[256,16]{1,0:T(8,128)(2,1)}), bf16[32,16]{1,0:T(8,128)(2,1)}) %reduce-scatter.60.cloned.1.call-update) | async-done | bytes 1040
  2279.6 63.8 %reduce-scatter.54.cloned.1.call-done = bf16[256,4]{1,0:T(8,128)(2,1)} async-done(((bf16[2048,4]{1,0:T(8,128)(2,1)}), bf16[256,4]{1,0:T(8,128)(2,1)}) %reduce-scatter.54.cloned.1.call-update) | async-done | bytes 2064
  2345.0 63.4 %reduce-scatter.52.cloned.1.call-done = bf16[256,4]{1,0:T(8,128)(2,1)} async-done(((bf16[2048,4]{1,0:T(8,128)(2,1)}), bf16[256,4]{1,0:T(8,128)(2,1)}) %reduce-scatter.52.cloned.1.call-update) | async-done | bytes 2064
  2409.9 68.9 %reduce-scatter.38.cloned.1.call-done = bf16[256,512]{1,0:T(8,128)(2,1)} async-done(((bf16[2048,512]{1,0:T(8,128)(2,1)}), bf16[256,512]{1,0:T(8,128)(2,1)}) %reduce-scatter.38.cloned.1.call-update) | async-done | bytes 262160 | tf_op jit(solution)/shard_map/reduce_scatter | solution.py:339
  2480.6 68.8 %reduce-scatter.36.cloned.1.call-done = bf16[256,512]{1,0:T(8,128)(2,1)} async-done(((bf16[2048,512]{1,0:T(8,128)(2,1)}), bf16[256,512]{1,0:T(8,128)(2,1)}) %reduce-scatter.36.cloned.1.call-update) | async-done | bytes 262160 | tf_op jit(solution)/shard_map/reduce_scatter | solution.py:336
  2551.3 89.0 %reduce-scatter.44.cloned.1.call-done = bf16[256,1024]{1,0:T(8,128)(2,1)} async-done(((bf16[2048,1024]{1,0:T(8,128)(2,1)}), bf16[256,1024]{1,0:T(8,128)(2,1)}) %reduce-scatter.44.cloned.1.call-update) | async-done | bytes 524304 | tf_op jit(solution)/shard_map/reduce_scatter | solution.py:354
  2642.4 89.1 %reduce-scatter.40.cloned.1.call-done = bf16[256,1024]{1,0:T(8,128)(2,1)} async-done(((bf16[2048,1024]{1,0:T(8,128)(2,1)}), bf16[256,1024]{1,0:T(8,128)(2,1)}) %reduce-scatter.40.cloned.1.call-update) | async-done | bytes 524304 | tf_op jit(solution)/shard_map/reduce_scatter | solution.py:342
  2733.6 44.9 %reduce-scatter.34.cloned.1.call-done = bf16[256,2048]{1,0:T(8,128)(2,1)} async-done(((bf16[1024,2048]{1,0:T(8,128)(2,1)}), bf16[256,2048]{1,0:T(8,128)(2,1)}) %reduce-scatter.34.cloned.1.call-update) | async-done | bytes 1048592 | tf_op jit(solution)/shard_map/reduce_scatter | solution.py:325
  2780.7 42.2 %all-reduce.28 = (f32[2048]{0:T(1024)}, f32[16]{0:T(128)}, f32[16]{0:T(128)}, f32[256]{0:T(256)}, f32[2048]{0:T(1024)}) all-reduce(f32[2048]{0:T(1024)S(1)} %get-tuple-element.756, f32[16]{0:T(128)S(1)} %multiply_dynamic-update-slice_fusion, f32[16]{0:T(128)S(1)} %dynamic_update_slice.68, ...), channel_id=1, replica_groups=mesh['dp'=8,'tensor'=4] {'dp','tensor'}, use_global_device_ids=true, to_apply=%region_31.33 | all-reduce | flops 4384 | bytes 35072 | tf_op jit(solution)/shard_map/psum | solution.py:382
  2822.9 48.4 %reduce-scatter.42.cloned.1.call-done = bf16[256,1024]{1,0:T(8,128)(2,1)} async-done(((bf16[2048,1024]{1,0:T(8,128)(2,1)}), bf16[256,1024]{1,0:T(8,128)(2,1)}) %reduce-scatter.42.cloned.1.call-update) | async-done | bytes 524304 | tf_op jit(solution)/shard_map/reduce_scatter | solution.py:345
  (1710 shorter events, 1717.1 us)
Async XLA Ops:
  13.3 164.5 %all-gather.19.cloned.1.call-start = ((), (), s32[]{:S(2)}) async-start(), calls=%async_computation.20 | async-start | bytes 2359296 | tf_op jit(solution)/shard_map/all_gather | solution.py:188
  14.0 211.2 %all-gather.17.cloned.1.call-start = ((), (), s32[]{:S(2)}) async-start(), calls=%async_computation.19 | async-start | bytes 4718592 | tf_op jit(solution)/shard_map/all_gather | solution.py:190
  14.6 725.5 %all-gather.21.cloned.1.call-start = ((), (), s32[]{:S(2)}) async-start(), calls=%async_computation.21 | async-start | bytes 4718592 | tf_op jit(solution)/shard_map/all_gather | solution.py:191
  15.2 737.8 %all-gather.23.cloned.1.call-start = ((), (), s32[]{:S(2)}) async-start(), calls=%async_computation.22 | async-start | bytes 4718592 | tf_op jit(solution)/shard_map/all_gather | solution.py:194
  15.8 817.1 %reduce-scatter.28.cloned.1.call-start = ((), (), s32[]{:S(2)}) async-start(), calls=%async_computation.23 | async-start | bytes 10485760 | tf_op jit(solution)/shard_map/reduce_scatter | solution.py:231
  762.8 276.8 %all-gather.31.cloned.1.call-start = ((), (), s32[]{:S(2)}) async-start(), calls=%async_computation.28 | async-start | bytes 5242880 | tf_op jit(solution)/shard_map/all_gather | solution.py:275
  765.2 274.4 %all-gather.29.cloned.1.call-start = ((), (), s32[]{:S(2)}) async-start(), calls=%async_computation.26 | async-start | bytes 6488064 | tf_op jit(solution)/shard_map/all_gather | solution.py:197
  766.0 358.7 %all-gather.27.cloned.1.call-start = ((), (), s32[]{:S(2)}) async-start(), calls=%async_computation.25 | async-start | bytes 6488064 | tf_op jit(solution)/shard_map/all_gather | solution.py:196
  766.5 393.0 %all-gather.25.cloned.1.call-start = ((), (), s32[]{:S(2)}) async-start(), calls=%async_computation.24 | async-start | bytes 5242880 | tf_op jit(solution)/shard_map/all_gather | solution.py:236
  836.1 418.4 %all-gather.33.cloned.1.call-start = ((), (), s32[]{:S(2)}) async-start(), calls=%async_computation.29 | async-start | bytes 6488064 | tf_op jit(solution)/shard_map/all_gather | solution.py:269
  938.5 404.9 %reduce-scatter.32.cloned.1.call-start = ((), (), s32[]{:S(2)}) async-start(), calls=%async_computation.30 | async-start | bytes 10485760 | tf_op jit(solution)/shard_map/reduce_scatter | solution.py:284
  1395.1 829.3 %reduce-scatter.46.cloned.1.call-start = ((), (), s32[]{:S(2)}) async-start(), calls=%async_computation.38 | async-start | bytes 6488064 | tf_op jit(solution)/shard_map/reduce_scatter | solution.py:366
  1406.2 820.6 %reduce-scatter.48.cloned.1.call-start = ((), (), s32[]{:S(2)}) async-start(), calls=%async_computation.39 | async-start | bytes 6488064 | tf_op jit(solution)/shard_map/reduce_scatter | solution.py:369
  1418.9 810.3 %reduce-scatter.50.cloned.1.call-start = ((), (), s32[]{:S(2)}) async-start(), calls=%async_computation.40 | async-start | bytes 6488064 | tf_op jit(solution)/shard_map/reduce_scatter | solution.py:372
  1437.5 794.3 %reduce-scatter.58.cloned.1.call-start = ((), (), s32[]{:S(2)}) async-start(), calls=%async_computation.44 | async-start | bytes 36864
  2111.8 166.4 %reduce-scatter.60.cloned.1.call-start = ((), (), s32[]{:S(2)}) async-start(), calls=%async_computation.45 | async-start | bytes 73728
  2113.1 230.4 %reduce-scatter.54.cloned.1.call-start = ((), (), s32[]{:S(2)}) async-start(), calls=%async_computation.42 | async-start | bytes 589824
  2117.3 291.1 %reduce-scatter.52.cloned.1.call-start = ((), (), s32[]{:S(2)}) async-start(), calls=%async_computation.41 | async-start | bytes 589824
  2121.3 357.6 %reduce-scatter.38.cloned.1.call-start = ((), (), s32[]{:S(2)}) async-start(), calls=%async_computation.34 | async-start | bytes 2359296 | tf_op jit(solution)/shard_map/reduce_scatter | solution.py:339
  2129.4 420.1 %reduce-scatter.36.cloned.1.call-start = ((), (), s32[]{:S(2)}) async-start(), calls=%async_computation.33 | async-start | bytes 2359296 | tf_op jit(solution)/shard_map/reduce_scatter | solution.py:336
  2136.8 503.5 %reduce-scatter.44.cloned.1.call-start = ((), (), s32[]{:S(2)}) async-start(), calls=%async_computation.37 | async-start | bytes 4718592 | tf_op jit(solution)/shard_map/reduce_scatter | solution.py:354
  2145.5 585.9 %reduce-scatter.40.cloned.1.call-start = ((), (), s32[]{:S(2)}) async-start(), calls=%async_computation.35 | async-start | bytes 4718592 | tf_op jit(solution)/shard_map/reduce_scatter | solution.py:342
  2168.8 609.6 %reduce-scatter.34.cloned.1.call-start = ((), (), s32[]{:S(2)}) async-start(), calls=%async_computation.32 | async-start | bytes 5242880 | tf_op jit(solution)/shard_map/reduce_scatter | solution.py:325
  2215.7 655.6 %reduce-scatter.42.cloned.1.call-start = ((), (), s32[]{:S(2)}) async-start(), calls=%async_computation.36 | async-start | bytes 4718592 | tf_op jit(solution)/shard_map/reduce_scatter | solution.py:345
  (132 other events, 8401.1 us)
Sparse Core Ops, SparseCore 0:
  10.2 53.4 all-gather.14
  101.0 49.6 all-gather.18
  152.7 72.4 all-gather.16
  227.2 72.4 all-gather.20
  301.7 72.0 all-gather.22
  762.9 69.9 reduce-scatter.27
  872.1 151.7 all-gather.28
  1026.1 98.4 all-gather.26
  1161.8 92.6 all-gather.32
  1273.4 69.9 reduce-scatter.31
  1345.8 44.4 reduce-scatter.29
  1433.7 110.1 reduce-scatter.45
  1547.8 109.6 reduce-scatter.47
  1661.5 110.0 reduce-scatter.49
  2104.1 53.5 reduce-scatter.57
  2161.0 52.5 reduce-scatter.55
  2217.9 60.2 reduce-scatter.59
  2282.5 60.8 reduce-scatter.53
  2347.4 60.9 reduce-scatter.51
  2412.2 66.6 reduce-scatter.37
  2482.8 66.6 reduce-scatter.35
  2553.4 86.8 reduce-scatter.43
  2643.8 87.6 reduce-scatter.39
  2782.1 89.1 reduce-scatter.41
  (5 shorter events, 178.6 us)
